TPU v7x, 64 devices: a 2x2x8 block of a 4x4x8 slice. The times are simulated.
64 devices in a mesh: dp: 4 (over x, y), tp: 16 (over z, core).
Axes of the slice: x: 2, y: 2, z: 8, core: 2. Of those that a mesh axis runs over, the one named last changes fastest.
The devices are a block of a 4x4x8 slice.
Arguments:
- hidden: bfloat16 [32, 16, 3072], P('dp'), parts along dimension 0
- norm_w: bfloat16 [3072], replicated
- embedding: bfloat16 [256000, 3072], P('tp')
- draft_ids: int32 [32, 16], P('dp'), parts along dimension 0
Outputs:
- output 1: float32 [32, 16], P('dp'), parts along dimension 0
- output 2: float32 [32, 16], P('dp'), parts along dimension 0
There are 4 independent parts. A program takes and returns all parts, laid end to end along the dimension named above; an argument that names none is the same for every part.
All inputs are finite; a program needn't handle non-finite values.
Results may differ from a plain program's by a relative error of at most 0.001.
Values sent between devices are 32-bit elements.
A program may use at most 768 MiB of HBM per device.

v0:
```python
import jax
import jax.numpy as jnp
from jax import lax
from jax.sharding import PartitionSpec as P, NamedSharding

EPS = 1e-6


def solution(mesh):
    def local_part(hidden, norm_w, embedding, draft_ids):
        shard_rows = embedding.shape[0]
        offset = lax.axis_index("tp") * shard_rows
        x_float = hidden.astype(jnp.float32)
        mean_sq = jnp.mean(x_float * x_float, axis=-1, keepdims=True)
        normed = (x_float * lax.rsqrt(mean_sq + EPS) * (1.0 + norm_w.astype(jnp.float32))).astype(jnp.bfloat16)
        logits = jnp.einsum("bgd,vd->bgv", normed, embedding, preferred_element_type=jnp.float32)
        local_max = jnp.max(logits, axis=-1)
        row_max = lax.pmax(local_max, "tp")
        exp_shift = jnp.exp(logits - row_max[..., None])
        exp_total = lax.psum(jnp.sum(exp_shift, axis=-1), "tp")
        weighted = lax.psum(jnp.sum(exp_shift * logits, axis=-1), "tp")
        local_ids = draft_ids - offset
        is_owned = (local_ids >= 0) & (local_ids < shard_rows)
        safe_ids = jnp.clip(local_ids, 0, shard_rows - 1)
        local_pick = jnp.take_along_axis(logits, safe_ids[..., None], axis=-1)[..., 0]
        picked = lax.psum(jnp.where(is_owned, local_pick, 0.0), "tp")
        log_norm = row_max + jnp.log(exp_total)
        return picked - log_norm, log_norm - weighted / exp_total

    return jax.shard_map(local_part, mesh=mesh, in_specs=(P("dp", None, None), P(None), P("tp", None), P("dp", None)), out_specs=(P("dp", None), P("dp", None)), check_vma=False)
```

profile of v0, /device:TPU:22, one launch (start us, length us, event | category | flops | bytes accessed | tf_op | source)
XLA Modules:
  0.0 129.5 jit_solution(6341686395649224643)
XLA Ops:
  0.6 1.3 %fusion.3 = f32[8,16]{1,0:T(8,128)S(1)} fusion(bf16[8,16,3072]{2,1,0:T(8,128)(2,1)} %param.4), kind=kLoop, calls=%fused_computation.8 | loop fusion | flops 1179520 | bytes 786944 | tf_op jit(solution)/shard_map/reduce_sum | solution.py:14
  2.0 0.7 fusion.14
  2.7 0.1 reshape.39
  2.8 0.7 convert_add_fusion
  3.5 41.9 %fusion.16 = (f32[8,16]{1,0:T(8,128)S(1)}, f32[8,16,16000]{2,1,0:T(8,128)}) fusion(bf16[16000,3072]{1,0:T(8,128)(2,1)} %param.6, bf16[8,16,3072]{2,1,0:T(8,128)(2,1)} %param.4, f32[3072]{0:T(1024)S(1)} %convert_add_fusion, f32[8,16]{1,0:T(8,128)S(1)} %add_rsqrt_fusion), kind=kOutput, calls=%fused_computation.30 | convolution fusion | flops 12586532864 | bytes 107295744 | tf_op jit(solution)/shard_map/bgd,vd->bgv/dot_general | solution.py:16
  45.4 0.0 copy-start
  45.4 30.3 %pmax.7 = f32[8,16]{1,0:T(8,128)S(1)} all-reduce(f32[8,16]{1,0:T(8,128)S(1)} %get-tuple-element.9), channel_id=1, replica_groups=mesh['dp'=4,'tp'=16] {'tp'}, use_global_device_ids=true, to_apply=%region_3.0 | all-reduce | flops 128 | bytes 1024 | tf_op jit(solution)/shard_map/pmax | solution.py:18
  75.8 2.3 %gather_fusion = f32[128]{0:T(128)S(1)} fusion(f32[8,16,16000]{2,1,0:T(8,128)} %get-tuple-element.10, s32[128]{0:T(128)S(1)} %reshape.39), kind=kCustom, calls=%fused_computation | custom fusion | bytes 2560 | tf_op jit(solution)/shard_map/jit(take_along_axis)/gather | solution.py:25
  78.0 5.0 %multiply_reduce_fusion = (f32[8,16]{1,0:T(8,128)S(1)}, f32[8,16]{1,0:T(8,128)S(1)}) fusion(f32[8,16,16000]{2,1,0:T(8,128)} %get-tuple-element.10, f32[8,16]{1,0:T(8,128)S(1)} %pmax.7), kind=kLoop, calls=%fused_computation.3 | loop fusion | flops 8191744 | bytes 8193536 | tf_op jit(solution)/shard_map/reduce_sum | solution.py:21
  83.0 0.1 gather.7
  83.1 0.0 copy-done
  83.1 45.8 %all-reduce = (f32[8,16]{1,0:T(8,128)S(1)}, f32[8,16]{1,0:T(8,128)S(1)}, f32[8,16]{1,0:T(8,128)S(1)}) all-reduce(f32[8,16]{1,0:T(8,128)S(1)} %select_select_fusion, f32[8,16]{1,0:T(8,128)S(1)} %get-tuple-element.3, f32[8,16]{1,0:T(8,128)S(1)} %get-tuple-element.2), channel_id=1, replica_groups=mesh['dp'=4,'tp'=16] {'tp'}, use_global_device_ids=true, to_apply=%region_1.0 | all-reduce | flops 384 | bytes 3072 | tf_op jit(solution)/shard_map/psum | solution.py:26
  128.9 0.6 divide_subtract_fusion
  (6 shorter events, 0.0 us)
Async XLA Ops:
  45.4 37.7 %copy-start = (s32[8,16]{1,0:T(8,128)S(1)}, s32[8,16]{1,0:T(8,128)}, u32[]{:S(2)}) copy-start(s32[8,16]{1,0:T(8,128)} %param.7) | copy-start | bytes 1540
where the time goes:
time: 130 us
  blocking collectives  76.1 us (59%)
  matrix products  41.9 us (32%)
  other arithmetic  8.39 us (6%)
  local copies, waits for them, and re-layouts  2.43 us (2%)
    psum x1, blocking collectives, local_part(): picked = lax.psum(jnp.where(is_owned, local_pick, 0.0), 'tp')  45.8 us
    dot_general x1, matrix products, local_part(): jnp.einsum('bgd,vd->bgv', normed, embedding, preferred_element_type=jnp.f...  41.9 us
    pmax x1, blocking collectives, local_part(): row_max = lax.pmax(local_max, 'tp')  30.3 us
    reduce_sum x1, other arithmetic, local_part(): weighted = lax.psum(jnp.sum(exp_shift * logits, axis=-1), 'tp')  4.98 us

commit v1 on v0

v1 whole, which is shorter than its diff:
```python
import functools

import jax
import jax.numpy as jnp
from jax import lax
from jax.experimental import pallas as pl
from jax.experimental.pallas import tpu as pltpu
from jax.sharding import PartitionSpec as P

EPS = 1e-6
MESH = pl.DeviceIdType.MESH
ROWS = 800
SLOTS = 8
HALF = ROWS // 2
LANES = 128
SUB = 8


def _peer(rank):
    return {"tp": rank}


def _stats_update(z, first_row, ids, stats):
    top, total, weighted, picked = stats
    rows, width = z.shape
    cube = z.reshape(rows // SUB, SUB, width)
    new_top = jnp.maximum(top, jnp.max(cube, axis=0))
    scale = jnp.exp(top - new_top)
    probs = jnp.exp(cube - new_top[None])
    total = total * scale + jnp.sum(probs, axis=0)
    weighted = weighted * scale + jnp.sum(probs * cube, axis=0)
    row_ids = lax.broadcasted_iota(jnp.int32, (rows, width), 0) + first_row
    hit = jnp.where(row_ids == ids, z, 0.0)
    picked = picked + jnp.sum(hit.reshape(rows // SUB, SUB, width), axis=0)
    return new_top, total, weighted, picked


def _kernel(tp, shard_rows, hidden_hbm, gain_ref, ids_ref, emb_hbm, out_ref, hid, wts, ring, even, odd, mine, board, hid_sem, ring_sem, send_sem, recv_sem):
    me = lax.axis_index("tp")
    chunks = shard_rows // ROWS
    depth = wts.shape[0]

    hid_copy = pltpu.make_async_copy(hidden_hbm, hid, hid_sem)
    hid_copy.start()

    def chunk_copy(idx, slot):
        return pltpu.make_async_copy(emb_hbm.at[pl.ds(pl.multiple_of(idx * ROWS, ROWS), ROWS)], ring.at[slot], ring_sem.at[slot])

    for idx in range(min(SLOTS, chunks)):
        chunk_copy(idx, idx).start()

    barrier = pltpu.get_barrier_semaphore()
    for step in range(1, tp):
        pl.semaphore_signal(barrier, inc=1, device_id=_peer(lax.rem(me + step, tp)), device_id_type=MESH)

    hid_copy.wait()
    gain = 1.0 + gain_ref[...].astype(jnp.float32)
    x = hid[...].astype(jnp.float32)
    mean_sq = jnp.sum(x * x, axis=-1, keepdims=True) / depth
    normed = x * lax.rsqrt(mean_sq + EPS) * gain
    wts[...] = normed.T.astype(jnp.bfloat16)

    ids = ids_ref[...] - me * shard_rows

    low = jnp.full((SUB, LANES), jnp.finfo(jnp.float32).min, jnp.float32)
    zero = jnp.zeros((SUB, LANES), jnp.float32)

    def multiply(idx, dst):
        slot = lax.rem(idx, SLOTS)
        chunk_copy(idx, slot).wait()
        stationary = wts[...]
        for part in range(2):
            rows = slice(part * HALF, (part + 1) * HALF)
            dst[rows] = jnp.dot(ring[slot, rows], stationary, preferred_element_type=jnp.float32)

    def refill(idx):
        @pl.when(idx + SLOTS < chunks)
        def _():
            chunk_copy(idx + SLOTS, lax.rem(idx, SLOTS)).start()

    def reduce(idx, src, stats):
        return _stats_update(src[...], idx * ROWS, ids, stats)

    multiply(0, even)
    refill(0)

    def body(pair, stats):
        idx = 2 * pair
        multiply(idx + 1, odd)
        stats = reduce(idx, even, stats)
        refill(idx + 1)
        multiply(idx + 2, even)
        stats = reduce(idx + 1, odd, stats)
        refill(idx + 2)
        return stats

    stats = lax.fori_loop(0, (chunks - 1) // 2, body, (low, zero, zero, zero))
    last = even
    if chunks % 2 == 0:
        multiply(chunks - 1, odd)
        stats = reduce(chunks - 2, even, stats)
        last = odd
    stats = reduce(chunks - 1, last, stats)

    top, total, weighted, picked = stats
    best = jnp.max(top, axis=0, keepdims=True)
    scale = jnp.exp(top - best)
    mine[0:1] = best
    mine[1:2] = jnp.sum(total * scale, axis=0, keepdims=True)
    mine[2:3] = jnp.sum(weighted * scale, axis=0, keepdims=True)
    mine[3:4] = jnp.sum(picked, axis=0, keepdims=True)
    mine[4:8] = jnp.zeros((4, LANES), jnp.float32)

    pl.semaphore_wait(barrier, tp - 1)

    def send(step):
        return pltpu.make_async_remote_copy(
            src_ref=mine, dst_ref=board.at[me], send_sem=send_sem.at[step], recv_sem=recv_sem.at[me],
            device_id=_peer(lax.rem(me + step, tp)), device_id_type=MESH)

    def receive(step):
        rank = lax.rem(me + step, tp)
        return pltpu.make_async_remote_copy(
            src_ref=mine, dst_ref=board.at[rank], send_sem=send_sem.at[step], recv_sem=recv_sem.at[rank],
            device_id=_peer(rank), device_id_type=MESH)

    for step in range(1, tp):
        send(step).start()
    board[me] = mine[...]
    for step in range(1, tp):
        receive(step).wait_recv()
    for step in range(1, tp):
        send(step).wait_send()

    every = board[...]
    tops = every[:, 0]
    row_max = jnp.max(tops, axis=0, keepdims=True)
    scale = jnp.exp(tops - row_max)
    exp_total = jnp.sum(every[:, 1] * scale, axis=0, keepdims=True)
    weighted = jnp.sum(every[:, 2] * scale, axis=0, keepdims=True)
    picked = jnp.sum(every[:, 3], axis=0, keepdims=True)
    log_norm = row_max + jnp.log(exp_total)
    out_ref[0:1] = picked - log_norm
    out_ref[1:2] = log_norm - weighted / exp_total


def solution(mesh):
    tp = mesh.shape["tp"]

    def local_part(hidden, norm_w, embedding, draft_ids):
        seqs, drafts, depth = hidden.shape
        positions = seqs * drafts
        shard_rows = embedding.shape[0]
        vmem = pl.BlockSpec(memory_space=pltpu.VMEM)
        hbm = pl.BlockSpec(memory_space=pl.ANY)
        out = pl.pallas_call(
            functools.partial(_kernel, tp, shard_rows),
            out_shape=jax.ShapeDtypeStruct((2, positions), jnp.float32),
            in_specs=[hbm, vmem, vmem, hbm],
            out_specs=vmem,
            scratch_shapes=[
                pltpu.VMEM((positions, depth), jnp.bfloat16),
                pltpu.VMEM((depth, positions), jnp.bfloat16),
                pltpu.VMEM((SLOTS, ROWS, depth), jnp.bfloat16),
                pltpu.VMEM((ROWS, positions), jnp.float32),
                pltpu.VMEM((ROWS, positions), jnp.float32),
                pltpu.VMEM((SUB, positions), jnp.float32),
                pltpu.VMEM((tp, SUB, positions), jnp.float32),
                pltpu.SemaphoreType.DMA,
                pltpu.SemaphoreType.DMA((SLOTS,)),
                pltpu.SemaphoreType.DMA((tp,)),
                pltpu.SemaphoreType.DMA((tp,)),
            ],
            compiler_params=pltpu.CompilerParams(collective_id=0, has_side_effects=True, vmem_limit_bytes=62 * 2**20),
            name="vocab_head",
        )(hidden.reshape(positions, depth), norm_w.reshape(1, depth), draft_ids.reshape(1, positions), embedding)
        return out[0].reshape(seqs, drafts), out[1].reshape(seqs, drafts)

    return jax.shard_map(local_part, mesh=mesh, in_specs=(P("dp", None, None), P(None), P("tp", None), P("dp", None)), out_specs=(P("dp", None), P("dp", None)), check_vma=False)
```

time: 130 us -> 58.8 us (0.45)
  the two profiles are of different devices: /device:TPU:22 before, /device:TPU:21 now
where the time goes in v1:
time: 58.8 us; the launch traced here: 58.6 us
  Pallas kernels  53.3 us (91%)
  local copies, waits for them, and re-layouts  4.67 us (8%)
  between operations  0.64 us (1%)
    pallas_call x1, Pallas kernels, local_part(): pl.pallas_call(functools.partial(_kernel, tp, shard_rows), out_shape=jax....  53.3 us
    another operation x2, local copies, waits for them, and re-layouts, local_part(): return (out[0].reshape(seqs, drafts), out[1].reshape(seqs, drafts))  1.35 us
    reshape x1, local copies, waits for them, and re-layouts, local_part(): norm_w.reshape(1, depth)  1.29 us
    reshape x1, local copies, waits for them, and re-layouts, local_part(): draft_ids.reshape(1, positions)  1.28 us

profile of v1, /device:TPU:21, one launch (start us, length us, event | category | flops | bytes accessed | tf_op | source)
XLA Modules:
  0.0 58.6 jit_solution(16546569584416677220)
XLA Ops:
  0.6 1.3 %reshape.15.ids_ref = s32[1,128]{1,0:T(1,128)} reshape(s32[8,16]{1,0:T(8,128)} %param.7) | data formatting | bytes 1024 | tf_op jit(solution)/shard_map/reshape | solution.py:176
  1.9 1.3 %reshape.14.gain_ref = bf16[1,3072]{1,0:T(2,128)(2,1)} reshape(bf16[3072]{0:T(1024)(128)(2,1)} %param.5) | data formatting | bytes 12288 | tf_op jit(solution)/shard_map/reshape | solution.py:176
  3.2 53.3 %vocab_head.1 = f32[2,128]{1,0:T(2,128)} custom-call(bf16[128,3072]{1,0:T(8,128)(2,1)} %bitcast.1, bf16[1,3072]{1,0:T(2,128)(2,1)} %reshape.14.gain_ref, s32[1,128]{1,0:T(1,128)} %reshape.15.ids_ref, bf16[16000,3072]{1,0:T(8,128)(2,1)} %emb_hbm.1), custom_call_target="tpu_custom_call" | custom-call | tf_op jit(solution)/shard_map/vocab_head/pallas_call | solution.py:156
  56.5 0.8 %slice_reduce_fusion = (f32[128]{0:T(128)S(1)}, f32[128]{0:T(128)S(1)}) fusion(f32[2,128]{1,0:T(2,128)} %vocab_head.1), kind=kLoop, calls=%fused_computation | loop fusion | bytes 2048 | tf_op jit(solution)/shard_map/slice | solution.py:177
  57.3 0.7 %reshape_squeeze.7 = f32[8,16]{1,0:T(8,128)} reshape(f32[128]{0:T(128)S(1)} %get-tuple-element.2) | data formatting | bytes 1024 | tf_op jit(solution)/shard_map/reshape;squeeze | solution.py:177
  57.9 0.7 %reshape_squeeze.6 = f32[8,16]{1,0:T(8,128)} reshape(f32[128]{0:T(128)S(1)} %get-tuple-element.3) | data formatting | bytes 1024 | tf_op jit(solution)/shard_map/reshape;squeeze | solution.py:177

commit v2 on v1

--- a/solution.py
+++ b/solution.py
@@ -35,32 +35,40 @@
     return new_top, total, weighted, picked
 
 
-def _kernel(tp, shard_rows, hidden_hbm, gain_ref, ids_ref, emb_hbm, out_ref, hid, wts, ring, even, odd, mine, board, hid_sem, ring_sem, send_sem, recv_sem):
+def _kernel(tp, hidden_hbm, gain_hbm, ids_hbm, emb_hbm, lp_ref, ent_ref, hid, gain_vm, ids_vm, wts, ring, even, odd, mine, board, hid_sem, gain_sem, ids_sem, ring_sem, send_sem, recv_sem):
     me = lax.axis_index("tp")
+    shard_rows, depth = emb_hbm.shape
     chunks = shard_rows // ROWS
-    depth = wts.shape[0]
+    seqs, drafts = lp_ref.shape
 
     hid_copy = pltpu.make_async_copy(hidden_hbm, hid, hid_sem)
-    hid_copy.start()
+    gain_copy = pltpu.make_async_copy(gain_hbm, gain_vm, gain_sem)
+    ids_copy = pltpu.make_async_copy(ids_hbm, ids_vm, ids_sem)
+    hid_copy.start(priority=0)
+    gain_copy.start(priority=0)
+    ids_copy.start(priority=0)
 
     def chunk_copy(idx, slot):
         return pltpu.make_async_copy(emb_hbm.at[pl.ds(pl.multiple_of(idx * ROWS, ROWS), ROWS)], ring.at[slot], ring_sem.at[slot])
 
     for idx in range(min(SLOTS, chunks)):
-        chunk_copy(idx, idx).start()
+        chunk_copy(idx, idx).start(priority=1)
 
     barrier = pltpu.get_barrier_semaphore()
     for step in range(1, tp):
         pl.semaphore_signal(barrier, inc=1, device_id=_peer(lax.rem(me + step, tp)), device_id_type=MESH)
 
+    gain_copy.wait()
+    ids_copy.wait()
     hid_copy.wait()
-    gain = 1.0 + gain_ref[...].astype(jnp.float32)
+    gain = 1.0 + gain_vm[...].astype(jnp.float32)[None]
     x = hid[...].astype(jnp.float32)
     mean_sq = jnp.sum(x * x, axis=-1, keepdims=True) / depth
     normed = x * lax.rsqrt(mean_sq + EPS) * gain
     wts[...] = normed.T.astype(jnp.bfloat16)
 
-    ids = ids_ref[...] - me * shard_rows
+    grid_ids = ids_vm[...] - me * shard_rows
+    ids = jnp.concatenate([grid_ids[seq:seq + 1] for seq in range(seqs)], axis=1)
 
     low = jnp.full((SUB, LANES), jnp.finfo(jnp.float32).min, jnp.float32)
     zero = jnp.zeros((SUB, LANES), jnp.float32)
@@ -76,7 +84,7 @@
     def refill(idx):
         @pl.when(idx + SLOTS < chunks)
         def _():
-            chunk_copy(idx + SLOTS, lax.rem(idx, SLOTS)).start()
+            chunk_copy(idx + SLOTS, lax.rem(idx, SLOTS)).start(priority=1)
 
     def reduce(idx, src, stats):
         return _stats_update(src[...], idx * ROWS, ids, stats)
@@ -140,8 +148,12 @@
     weighted = jnp.sum(every[:, 2] * scale, axis=0, keepdims=True)
     picked = jnp.sum(every[:, 3], axis=0, keepdims=True)
     log_norm = row_max + jnp.log(exp_total)
-    out_ref[0:1] = picked - log_norm
-    out_ref[1:2] = log_norm - weighted / exp_total
+    log_prob = picked - log_norm
+    entropy = log_norm - weighted / exp_total
+    for seq in range(seqs):
+        lanes = slice(seq * drafts, (seq + 1) * drafts)
+        lp_ref[seq:seq + 1] = log_prob[:, lanes]
+        ent_ref[seq:seq + 1] = entropy[:, lanes]
 
 
 def solution(mesh):
@@ -150,16 +162,18 @@
     def local_part(hidden, norm_w, embedding, draft_ids):
         seqs, drafts, depth = hidden.shape
         positions = seqs * drafts
-        shard_rows = embedding.shape[0]
         vmem = pl.BlockSpec(memory_space=pltpu.VMEM)
         hbm = pl.BlockSpec(memory_space=pl.ANY)
-        out = pl.pallas_call(
-            functools.partial(_kernel, tp, shard_rows),
-            out_shape=jax.ShapeDtypeStruct((2, positions), jnp.float32),
-            in_specs=[hbm, vmem, vmem, hbm],
-            out_specs=vmem,
+        grid = jax.ShapeDtypeStruct((seqs, drafts), jnp.float32)
+        return pl.pallas_call(
+            functools.partial(_kernel, tp),
+            out_shape=(grid, grid),
+            in_specs=[hbm] * 4,
+            out_specs=(vmem, vmem),
             scratch_shapes=[
                 pltpu.VMEM((positions, depth), jnp.bfloat16),
+                pltpu.VMEM((depth,), jnp.bfloat16),
+                pltpu.VMEM((seqs, drafts), jnp.int32),
                 pltpu.VMEM((depth, positions), jnp.bfloat16),
                 pltpu.VMEM((SLOTS, ROWS, depth), jnp.bfloat16),
                 pltpu.VMEM((ROWS, positions), jnp.float32),
@@ -167,13 +181,14 @@
                 pltpu.VMEM((SUB, positions), jnp.float32),
                 pltpu.VMEM((tp, SUB, positions), jnp.float32),
                 pltpu.SemaphoreType.DMA,
+                pltpu.SemaphoreType.DMA,
+                pltpu.SemaphoreType.DMA,
                 pltpu.SemaphoreType.DMA((SLOTS,)),
                 pltpu.SemaphoreType.DMA((tp,)),
                 pltpu.SemaphoreType.DMA((tp,)),
             ],
             compiler_params=pltpu.CompilerParams(collective_id=0, has_side_effects=True, vmem_limit_bytes=62 * 2**20),
             name="vocab_head",
-        )(hidden.reshape(positions, depth), norm_w.reshape(1, depth), draft_ids.reshape(1, positions), embedding)
-        return out[0].reshape(seqs, drafts), out[1].reshape(seqs, drafts)
+        )(hidden.reshape(positions, depth), norm_w, draft_ids, embedding)
 
     return jax.shard_map(local_part, mesh=mesh, in_specs=(P("dp", None, None), P(None), P("tp", None), P("dp", None)), out_specs=(P("dp", None), P("dp", None)), check_vma=False)

time: 58.8 us -> 47.9 us (0.81)
  Pallas kernels: 53.3 us -> 44.6 us
  local copies, waits for them, and re-layouts: 4.67 us -> 2.53 us
    pallas_call x1, Pallas kernels: 53.3 us -> 44.6 us  [local_part(): pl.pallas_call(functools.partial(_kernel, tp), out_shape=(grid, grid), in...]
    reshape x2 -> x0, local copies, waits for them, and re-layouts: 2.57 us -> none  [the longest x1 1.29 us: local_part(): norm_w.reshape(1, depth)]
    unnamed x0 -> x2, local copies, waits for them, and re-layouts: none -> 2.53 us
    another operation x2 -> x0, local copies, waits for them, and re-layouts: 1.35 us -> none  [local_part(): return (out[0].reshape(seqs, drafts), out[1].reshape(seqs, drafts))]
    slice x1 -> x0, local copies, waits for them, and re-layouts: 0.75 us -> none  [local_part(): return (out[0].reshape(seqs, drafts), out[1].reshape(seqs, drafts))]
where the time goes in v2:
time: 47.9 us; the launch traced here: 47.8 us
  Pallas kernels  44.6 us (93%)
  local copies, waits for them, and re-layouts  2.53 us (5%)
  between operations  0.64 us (1%)
    pallas_call x1, Pallas kernels, local_part(): pl.pallas_call(functools.partial(_kernel, tp), out_shape=(grid, grid), in...  44.6 us
    unnamed x2, local copies, waits for them, and re-layouts  2.53 us

profile of v2, /device:TPU:21, one launch (start us, length us, event | category | flops | bytes accessed | tf_op | source)
XLA Modules:
  0.0 47.8 jit_solution(16643595964920646820)
XLA Ops:
  0.6 44.6 %vocab_head.1 = (f32[8,16]{1,0:T(8,128)}, f32[8,16]{1,0:T(8,128)}) custom-call(bf16[128,3072]{1,0:T(8,128)(2,1)} %bitcast.1, bf16[3072]{0:T(1024)(128)(2,1)} %gain_hbm.1, s32[8,16]{1,0:T(8,128)} %ids_hbm.1, bf16[16000,3072]{1,0:T(8,128)(2,1)} %emb_hbm.1), custom_call_target="tpu_custom_call" | custom-call | tf_op jit(solution)/shard_map/vocab_head/pallas_call | solution.py:168
  45.3 1.3 %copy.8 = f32[8,16]{1,0:T(8,128)} copy(f32[8,16]{1,0:T(8,128)} %get-tuple-element.4) | data formatting | bytes 1024
  46.5 1.3 %copy.9 = f32[8,16]{1,0:T(8,128)} copy(f32[8,16]{1,0:T(8,128)} %get-tuple-element.5) | data formatting | bytes 1024
